TPU v7x, 32 devices: a whole 2x2x4 slice. The times are simulated.
32 devices in a mesh: groups: 2 (over y), seq: 4 (over x, core), tensor: 4 (over z).
Axes of the slice: x: 2, y: 2, z: 4, core: 2. Of those that a mesh axis runs over, the one named last changes fastest.
Arguments:
- hidden: bfloat16 [256, 4608], P(('groups', 'seq')), parts along dimension 0, may hold values from -6 to 6
- pre_gain: float32 [4608], replicated, may hold values from 0.25 to 1.75
- w_query: bfloat16 [4608, 4096], P(None, 'tensor'), may hold values from -0.09375 to 0.09375
- w_key: bfloat16 [4608, 2048], P(None, 'tensor'), may hold values from -0.09375 to 0.09375
- w_value: bfloat16 [4608, 2048], P(None, 'tensor'), may hold values from -0.09375 to 0.09375
- w_out: bfloat16 [4096, 4608], P('tensor'), may hold values from -0.125 to 0.125
- post_gain: float32 [4608], P('tensor'), may hold values from 0.25 to 1.75
- cache_pool: bfloat16 [512, 2, 128, 2048], P(('groups', 'seq'), None, None, 'tensor'), parts along dimension 0, may hold values from -6 to 6
- prompt_cache: bfloat16 [256, 2, 64, 2048], P('seq', None, None, 'tensor'), may hold values from -6 to 6
- task_ids: int32 [256], P('groups'), parts along dimension 0, may hold values from 0 to 255
- cache_lengths: int32 [256], P('groups'), parts along dimension 0, may hold values from 1 to 4096, as said below
- block_table: int32 [256, 32], P('groups'), parts along dimension 0, may hold values from -1 to 255, as said below
Outputs:
- layer_out: bfloat16 [256, 4608], P(('groups', 'seq'), 'tensor'), parts along dimension 0
- fresh_cache: bfloat16 [256, 2, 2048], P(('groups', 'seq'), None, 'tensor'), parts along dimension 0
There are 2 independent parts, one for each index of `groups`. A program takes and returns all parts, laid end to end along the dimension named above; an argument that names none is the same for every part. Nothing has to cross between parts.
Inputs may be any that keep to these rules, and one draw needn't show every extreme that they name: `cache_lengths`: each draw has a request with exactly 4096 cache tokens. block_table[r, j] is the page of cache_pool holding cache tokens j * 128 to (j + 1) * 128 - 1 of request r for j < ceil(cache_lengths[r] / 128), and -1 for the later j; no page is named twice.
All inputs are finite; a program needn't handle non-finite values.
Results may differ from a plain program's by a relative error of at most 0.018.
Values may be sent and summed in bfloat16 or wider, within the bound.
A program may use at most 128 MiB of HBM per device.

v0:
```python
import jax
import jax.numpy as jnp
from jax import lax
from jax.sharding import PartitionSpec as P

D = 4608
H = 32
HD = 128


cap_limit = 50.0


def rms_scale(values, gain):
    mean_square = jnp.mean(values * values, axis=-1, keepdims=True)
    return values * lax.rsqrt(mean_square + 1e-06) * gain


def rotate(values, position):
    half_dim = values.shape[-1] // 2
    frequency = 10000.0 ** (-jnp.arange(half_dim, dtype=jnp.float32) / half_dim)
    angles = position.astype(jnp.float32)[:, None] * frequency[None, :]
    cosine = jnp.cos(angles)[:, None, :]
    sines = jnp.sin(angles)[:, None, :]
    first_half = values[..., :half_dim]
    second_half = values[..., half_dim:]
    return jnp.concatenate(
        [first_half * cosine - second_half * sines, second_half * cosine + first_half * sines],
        axis=-1,
    )


def capped(raw_score, score_scale):
    return cap_limit * jnp.tanh(raw_score * score_scale / cap_limit)


def attend(query_block, block, live_mask, score_scale):
    count = block.shape[0]
    length = block.shape[2]
    kv_heads = query_block.shape[1]
    head_dim = query_block.shape[3]
    block_keys = block[:, 0].reshape(count, length, kv_heads, head_dim)
    block_values = block[:, 1].reshape(count, length, kv_heads, head_dim)
    raw_score = jnp.einsum(
        "nkgd,ntkd->nkgt", query_block, block_keys, preferred_element_type=jnp.float32
    )
    weight = jnp.where(live_mask[:, None, None, :], jnp.exp(capped(raw_score, score_scale)), 0.0)
    totals = jnp.sum(weight, axis=-1).reshape(count, -1)
    mixtures = jnp.einsum(
        "nkgt,ntkd->nkgd",
        weight.astype(jnp.bfloat16),
        block_values,
        preferred_element_type=jnp.float32,
    )
    return (totals, mixtures.reshape(count, -1))


def body(
    hidden,
    pre_gain,
    w_query,
    w_key,
    w_value,
    w_out,
    post_gain,
    cache_pool,
    prompt_cache,
    task_ids,
    cache_lengths,
    block_table,
):
    seq_index = lax.axis_index("seq")
    tensor_index = lax.axis_index("tensor")
    own_rows = hidden.shape[0]
    requests = task_ids.shape[0]
    pages_dev = cache_pool.shape[0]
    block_len = cache_pool.shape[2]
    kv_width = cache_pool.shape[3]
    head_dim = HD
    kv_heads = kv_width // head_dim
    query_heads = w_query.shape[1] // head_dim
    group_size = query_heads // kv_heads
    prompt_len = prompt_cache.shape[2]
    tasks_dev = prompt_cache.shape[0]
    score_scale = float(D // H) ** (-0.5)
    first_row = seq_index * own_rows
    own_lengths = lax.dynamic_slice_in_dim(cache_lengths, first_row, own_rows)
    normed = rms_scale(hidden.astype(jnp.float32), pre_gain).astype(jnp.bfloat16)
    position = prompt_len + own_lengths
    query_rows = rotate(
        jnp.dot(normed, w_query, preferred_element_type=jnp.float32).reshape(
            own_rows, query_heads, head_dim
        ),
        position,
    ).astype(jnp.bfloat16)
    key_new = rotate(
        jnp.dot(normed, w_key, preferred_element_type=jnp.float32).reshape(
            own_rows, kv_heads, head_dim
        ),
        position,
    ).astype(jnp.bfloat16)
    value_new = jnp.dot(normed, w_value, preferred_element_type=jnp.float32).astype(jnp.bfloat16)
    fresh_cache = jnp.stack([key_new.reshape(own_rows, kv_width), value_new], axis=1)
    queries = lax.all_gather(
        query_rows.reshape(own_rows, query_heads * head_dim), "seq", axis=0, tiled=True
    )
    page_ids = seq_index * pages_dev + jnp.arange(pages_dev)
    flat_table = block_table.reshape(-1)
    max_blocks = block_table.shape[1]
    matches = flat_table[None, :] == page_ids[:, None]
    entry_index = jnp.arange(flat_table.shape[0])
    page_used = jnp.any(matches, axis=1)
    found_entry = jnp.sum(jnp.where(matches, entry_index[None, :], 0), axis=1)
    page_owner = found_entry // max_blocks
    block_number = found_entry % max_blocks
    owner_hot = (page_owner[:, None] == jnp.arange(requests)[None, :]) & page_used[:, None]
    owner_length = jnp.sum(jnp.where(owner_hot, cache_lengths[None, :], 0), axis=1)
    valid_count = jnp.clip(owner_length - block_number * block_len, 0, block_len)
    page_query = jnp.dot(
        owner_hot.astype(jnp.bfloat16), queries, preferred_element_type=jnp.float32
    ).astype(jnp.bfloat16)
    page_query = page_query.reshape(pages_dev, kv_heads, group_size, head_dim)
    page_live = jnp.arange(block_len)[None, :] < valid_count[:, None]
    page_totals, page_mixtures = attend(page_query, cache_pool, page_live, score_scale)
    spread_hot = owner_hot.astype(jnp.float32).T
    totals = jnp.dot(spread_hot, page_totals, precision=lax.Precision.HIGHEST)
    mixtures = jnp.dot(spread_hot, page_mixtures, precision=lax.Precision.HIGHEST)
    local_task = task_ids - seq_index * tasks_dev
    is_owned = (local_task >= 0) & (local_task < tasks_dev)
    task_rows = prompt_cache[jnp.clip(local_task, 0, tasks_dev - 1)]
    all_query = queries.reshape(requests, kv_heads, group_size, head_dim)
    owned_live = jnp.broadcast_to(is_owned[:, None], (requests, prompt_len))
    prompt_totals, prompt_mixtures = attend(all_query, task_rows, owned_live, score_scale)
    totals = totals + prompt_totals
    mixtures = mixtures + prompt_mixtures
    totals, mixtures = (
        lax.psum_scatter(
            totals.astype(jnp.bfloat16), "seq", scatter_dimension=0, tiled=True
        ).astype(jnp.float32),
        lax.psum_scatter(
            mixtures.astype(jnp.bfloat16), "seq", scatter_dimension=0, tiled=True
        ).astype(jnp.float32),
    )
    own_query = query_rows.reshape(own_rows, kv_heads, group_size, head_dim)
    self_raw = jnp.sum(
        own_query.astype(jnp.float32) * key_new[:, :, None, :].astype(jnp.float32), axis=-1
    )
    self_weight = jnp.exp(capped(self_raw, score_scale))
    rounded = lax.optimization_barrier(self_weight.astype(jnp.bfloat16)).astype(jnp.float32)
    totals = totals + self_weight.reshape(own_rows, -1)
    self_mix = rounded[..., None] * value_new.reshape(own_rows, kv_heads, 1, head_dim).astype(
        jnp.float32
    )
    mixtures = mixtures + self_mix.reshape(own_rows, -1)
    attended = (mixtures.reshape(own_rows, query_heads, head_dim) / totals[..., None]).astype(
        jnp.bfloat16
    )
    projected = jnp.dot(
        attended.reshape(own_rows, query_heads * head_dim),
        w_out,
        preferred_element_type=jnp.float32,
    )
    cols_local = post_gain.shape[0]
    col_start = tensor_index * cols_local
    residual = lax.dynamic_slice_in_dim(hidden, col_start, cols_local, 1).astype(jnp.float32)
    whole_sum = lax.psum(projected.astype(jnp.bfloat16), "tensor").astype(jnp.float32)
    mean_square = jnp.mean(whole_sum * whole_sum, axis=1, keepdims=True)
    scaled = lax.dynamic_slice_in_dim(whole_sum, col_start, cols_local, 1) * lax.rsqrt(
        mean_square + 1e-06
    )
    layer_out = (residual + scaled * post_gain).astype(jnp.bfloat16)
    return (layer_out, fresh_cache)


def solution(mesh):
    return jax.shard_map(
        body,
        mesh=mesh,
        in_specs=(
            P(("groups", "seq"), None),
            P(),
            P(None, "tensor"),
            P(None, "tensor"),
            P(None, "tensor"),
            P("tensor", None),
            P("tensor"),
            P(("groups", "seq"), None, None, "tensor"),
            P("seq", None, None, "tensor"),
            P("groups"),
            P("groups"),
            P("groups", None),
        ),
        out_specs=(P(("groups", "seq"), "tensor"), P(("groups", "seq"), None, "tensor")),
        check_vma=False,
    )
```

profile of v0, /device:TPU:0, one launch (start us, length us, event | category | flops | bytes accessed | tf_op | source)
XLA Modules:
  0.0 237.8 jit_solution(1998318495962879514)
XLA Ops:
  7.2 0.0 reduce-scatter.7.cloned.1.call-start
  7.2 0.7 compare_select_fusion.1
  7.9 0.7 compare_and_fusion
  8.6 0.8 copy.81
  9.4 0.1 eq.32
  9.5 0.3 fusion.10
  9.8 0.3 compare_reduce_fusion
  10.1 1.1 fusion.11
  11.2 5.6 %convolution_bitcast_fusion = f32[4,8,8,128]{3,1,2,0:T(8,128)S(1)} fusion(bf16[4608,1024]{1,0:T(8,128)(2,1)} %param.14, bf16[32,4608]{1,0:T(8,128)(2,1)} %param.12, f32[4608]{0:T(1024)} %param.13, f32[32]{0:T(128)S(1)} %add_rsqrt_fusion.1), kind=kOutput, calls=%fused_computation.17 | convolution fusion | flops 302579712 | bytes 9881728 | tf_op jit(solution)/shard_map/dot_general | solution.py:91
  16.9 0.1 add_convert_fusion.2
  16.9 0.1 multiply_cosine_fusion
  17.1 0.1 subtract_convert_fusion
  17.2 0.1 pad_maximum_fusion
  17.3 7.2 %all_gather.3 = bf16[128,1024]{1,0:T(8,128)(2,1)S(1)} all-gather(bf16[32,1024]{1,0:T(8,128)(2,1)S(1)} %bitcast.48), channel_id=1, replica_groups=mesh['groups'=2,'seq'=4,'tensor'=4] {'seq'}, dimensions={0}, use_global_device_ids=true | all-gather | bytes 327680 | tf_op jit(solution)/shard_map/all_gather | solution.py:104
  24.5 0.2 reshape.222
  24.7 0.2 convolution_convert_fusion.1
  25.0 0.2 select_reduce_fusion
  25.2 11.2 %gather_fusion = bf16[128,2,64,512]{3,2,1,0:T(8,128)(2,1)} fusion(bf16[64,2,64,512]{3,2,1,0:T(8,128)(2,1)} %param.20, s32[1024]{0:T(1024)S(1)} %pad_clamp_fusion), kind=kCustom, calls=%fused_computation | custom fusion | bytes 33554944 | tf_op jit(solution)/shard_map/gather | solution.py:130
  36.3 11.7 %fusion.40 = (bf16[128,1,64,512]{3,2,1,0:T(8,128)(2,1)}, bf16[128,1,64,512]{3,2,1,0:T(8,128)(2,1)}) fusion(bf16[128,2,64,512]{3,2,1,0:T(8,128)(2,1)} %gather_fusion), kind=kLoop, calls=%fused_computation.79 | loop fusion | bytes 33554432 | tf_op jit(solution)/shard_map/slice | solution.py:43
  48.0 13.0 %copy.86 = bf16[128,1,64,512]{0,3,2,1:T(8,128)(2,1)} copy(bf16[128,1,64,512]{3,2,1,0:T(8,128)(2,1)} %get-tuple-element.21) | data formatting | bytes 16777216 | tf_op jit(solution)/shard_map/slice | solution.py:42
  61.0 12.0 %copy.87 = bf16[128,64,4,128]{3,1,2,0:T(8,128)(2,1)} copy(bf16[128,64,4,128]{0,3,2,1:T(8,128)(2,1)} %bitcast.41) | data formatting | bytes 16777216 | tf_op jit(solution)/shard_map/reshape;squeeze | solution.py:42
  73.0 8.0 %fusion.41 = (f32[128,4,2]{2,1,0:T(4,128)S(1)}, bf16[128,4,2,64]{3,2,1,0:T(2,128)(2,1)S(1)}) fusion(bf16[128,4,2,128]{3,2,1,0:T(2,128)(2,1)S(1)} %reshape.222, bf16[128,64,4,128]{3,1,2,0:T(8,128)(2,1)} %copy.87, pred[128]{0:T(512)(128)(4,1)S(1)} %compare_and_fusion), kind=kOutput, calls=%fused_computation.80 | convolution fusion | flops 17103872 | bytes 8786048 | tf_op jit(solution)/shard_map/nkgd,ntkd->nkgt/dot_general | solution.py:44
  81.0 0.1 copy.93
  81.1 0.1 reshape.220
  81.2 11.6 %fusion.39 = (bf16[64,1,128,512]{3,2,1,0:T(8,128)(2,1)}, bf16[64,1,128,512]{3,2,1,0:T(8,128)(2,1)}) fusion(bf16[64,2,128,512]{3,2,1,0:T(8,128)(2,1)} %param.19), kind=kLoop, calls=%fused_computation.78 | loop fusion | bytes 33554432 | tf_op jit(solution)/shard_map/slice | solution.py:43
  92.8 11.9 %copy.101 = bf16[64,1,128,512]{2,3,0,1:T(8,128)(2,1)} copy(bf16[64,1,128,512]{3,2,1,0:T(8,128)(2,1)} %get-tuple-element.19) | data formatting | bytes 16777216
  104.7 0.1 iota_compare_fusion
  104.8 5.8 %fusion.42 = (f32[64,4,2]{2,1,0:T(4,128)S(1)}, bf16[64,4,2,128]{3,2,1,0:T(2,128)(2,1)S(1)}) fusion(bf16[64,4,2,128]{3,2,1,0:T(2,128)(2,1)S(1)} %reshape.220, bf16[64,128,4,128]{1,3,2,0:T(8,128)(2,1)} %bitcast.39, pred[64,128]{1,0:T(8,128)(4,1)S(1)} %iota_compare_fusion), kind=kOutput, calls=%fused_computation.81 | convolution fusion | flops 17104384 | bytes 8660992 | tf_op jit(solution)/shard_map/nkgd,ntkd->nkgt/dot_general | solution.py:44
  110.6 0.1 copy.92
  110.7 0.2 fusion.9
  110.9 0.7 copy.99
  111.7 0.0 reduce-scatter.7.cloned.1.call-update
  111.7 0.2 reduce-scatter.5.cloned.1.call-start
  111.9 13.0 %copy.88 = bf16[128,1,64,512]{0,3,2,1:T(8,128)(2,1)} copy(bf16[128,1,64,512]{3,2,1,0:T(8,128)(2,1)} %get-tuple-element.20) | data formatting | bytes 16777216 | tf_op jit(solution)/shard_map/slice | solution.py:43
  124.9 12.0 %copy.89 = bf16[128,64,4,128]{3,1,2,0:T(8,128)(2,1)} copy(bf16[128,64,4,128]{0,3,2,1:T(8,128)(2,1)} %bitcast.42) | data formatting | bytes 16777216 | tf_op jit(solution)/shard_map/reshape;squeeze | solution.py:43
  136.9 5.6 %fusion.14 = f32[128,4,2,128]{3,2,1,0:T(2,128)S(1)} fusion(bf16[128,64,4,128]{3,1,2,0:T(8,128)(2,1)} %copy.89, bf16[128,4,2,64]{3,2,1,0:T(2,128)(2,1)S(1)} %get-tuple-element.31), kind=kOutput, calls=%fused_computation.28 | convolution fusion | flops 16777216 | bytes 9043968 | tf_op jit(solution)/shard_map/nkgt,ntkd->nkgd/dot_general | solution.py:49
  142.6 0.4 reshape.223
  143.0 11.9 %copy.102 = bf16[64,1,128,512]{2,3,0,1:T(8,128)(2,1)} copy(bf16[64,1,128,512]{3,2,1,0:T(8,128)(2,1)} %get-tuple-element.18) | data formatting | bytes 16777216
  154.9 7.8 %fusion.17 = f32[64,4,2,128]{3,2,1,0:T(2,128)S(1)} fusion(bf16[64,128,4,128]{1,3,2,0:T(8,128)(2,1)} %bitcast.40, bf16[64,4,2,128]{3,2,1,0:T(2,128)(2,1)S(1)} %get-tuple-element.33), kind=kOutput, calls=%fused_computation.34 | convolution fusion | flops 16777216 | bytes 8781824 | tf_op jit(solution)/shard_map/nkgt,ntkd->nkgd/dot_general | solution.py:49
  162.7 0.2 reshape.221
  163.0 1.2 fusion.4
  164.2 0.0 reduce-scatter.5.cloned.1.call-update
  164.2 0.0 all-reduce.2.cloned.1.call-start
  164.3 3.3 %fusion.35 = f32[32,512]{1,0:T(8,128)S(1)} fusion(bf16[4608,512]{1,0:T(8,128)(2,1)} %param.15, bf16[32,4608]{1,0:T(8,128)(2,1)S(1)} %copy-done, f32[4608]{0:T(1024)S(1)} %copy-done.1, f32[32]{0:T(128)S(1)} %add_rsqrt_fusion.1), kind=kOutput, calls=%fused_computation.76 | convolution fusion | flops 151584768 | bytes 5097600 | tf_op jit(solution)/shard_map/dot_general | solution.py:97
  167.6 0.1 multiply_subtract_fusion
  167.7 0.1 fusion.38
  167.8 0.4 multiply_reduce_fusion.1
  168.2 0.1 copy.90
  168.3 3.3 %convolution_convert_fusion.2 = bf16[32,512]{1,0:T(8,128)(2,1)S(1)} fusion(bf16[4608,512]{1,0:T(8,128)(2,1)} %param.16, bf16[32,4608]{1,0:T(8,128)(2,1)S(1)} %copy-done, f32[4608]{0:T(1024)S(1)} %copy-done.1, f32[32]{0:T(128)S(1)} %add_rsqrt_fusion.1), kind=kOutput, calls=%fused_computation.18 | convolution fusion | flops 151601152 | bytes 5064832 | tf_op jit(solution)/shard_map/dot_general | solution.py:102
  171.7 0.1 copy.91
  171.8 0.2 broadcast_multiply_fusion
  172.0 0.1 mul.214
  172.1 0.0 reduce-scatter.7.cloned.1.call-done
  172.2 0.8 copy.100
  172.9 0.1 copy.95
  173.0 13.0 %reduce-scatter.5.cloned.1.call-done = bf16[32,1024]{1,0:T(8,128)(2,1)} async-done(((bf16[128,1024]{1,0:T(8,128)(2,1)}), bf16[32,1024]{1,0:T(8,128)(2,1)}) %reduce-scatter.5.cloned.1.call-update) | async-done | bytes 65552 | tf_op jit(solution)/shard_map/reduce_scatter | solution.py:140
  186.0 0.1 div.60
  186.1 6.1 %convolution_convert_fusion = bf16[32,4608]{1,0:T(8,128)(2,1)} fusion(bf16[1024,4608]{1,0:T(8,128)(2,1)} %param.17, f32[4,8,8,128]{3,2,1,0:T(8,128)S(1)} %bitcast.44, f32[32,1024]{1,0:T(8,128)S(1)} %mul.214, bf16[32,1024]{1,0:T(8,128)(2,1)} %reduce-scatter.5.cloned.1.call-done), kind=kOutput, calls=%fused_computation.1 | convolution fusion | flops 302268416 | bytes 10059776 | tf_op jit(solution)/shard_map/dot_general | solution.py:158
  192.2 0.0 all-reduce.2.cloned.1.call-update
  192.3 0.7 copy.96
  193.0 35.3 %all-reduce.2.cloned.1.call-done = bf16[32,4608]{1,0:T(8,128)(2,1)} async-done(((bf16[32,4608]{1,0:T(8,128)(2,1)}), bf16[32,4608]{1,0:T(8,128)(2,1)}) %all-reduce.2.cloned.1.call-update) | async-done | bytes 294928 | tf_op jit(solution)/shard_map/psum | solution.py:166
  228.4 1.1 multiply_reduce_fusion
  229.5 1.0 convert_element_type.125
  230.5 0.7 add_convert_fusion
  (24 shorter events, 0.2 us)
Async XLA Ops:
  7.2 165.0 %reduce-scatter.7.cloned.1.call-start = ((), (), s32[]{:S(2)}) async-start(), calls=%async_computation.4 | async-start | bytes 40960
  11.2 5.7 %copy-start.3 = (s32[128]{0:T(128)S(1)}, s32[128]{0:T(128)}, u32[]{:S(2)}) copy-start(s32[128]{0:T(128)} %param.22) | copy-start | bytes 1540
  111.7 74.3 %reduce-scatter.5.cloned.1.call-start = ((), (), s32[]{:S(2)}) async-start(), calls=%async_computation.2 | async-start | bytes 327680 | tf_op jit(solution)/shard_map/reduce_scatter | solution.py:140
  154.9 9.3 %copy-start = (bf16[32,4608]{1,0:T(8,128)(2,1)S(1)}, bf16[32,4608]{1,0:T(8,128)(2,1)}, u32[]{:S(2)}) copy-start(bf16[32,4608]{1,0:T(8,128)(2,1)} %param.12) | copy-start | bytes 884740
  154.9 9.3 %copy-start.1 = (f32[4608]{0:T(1024)S(1)}, f32[4608]{0:T(1024)}, u32[]{:S(2)}) copy-start(f32[4608]{0:T(1024)} %param.13) | copy-start | bytes 55300
  164.2 64.2 %all-reduce.2.cloned.1.call-start = ((), (), s32[]{:S(2)}) async-start(), calls=%async_computation.3 | async-start | bytes 589824 | tf_op jit(solution)/shard_map/psum | solution.py:166
  186.1 44.4 %copy-start.2 = (f32[1152]{0:T(1024)S(1)}, f32[1152]{0:T(1024)}, u32[]{:S(2)}) copy-start(f32[1152]{0:T(1024)} %param.18) | copy-start | bytes 13828
Sparse Core Ops, SparseCore 0:
  111.8 21.1 reduce-scatter.6
  164.3 21.6 reduce-scatter.4
  192.4 35.9 all-reduce.1
where the time goes:
time: 240 us; the launch traced here: 238 us
  local copies, waits for them, and re-layouts  113 us (47%)
  waiting for transfers between devices  48.4 us (20%)
  matrix products  47.2 us (20%)
  between operations  14 us (6%)
  other arithmetic  7.5 us (3%)
  blocking collectives  7.22 us (3%)
    slice x3, local copies, waits for them, and re-layouts, attend(): block_values = block[:, 1].reshape(count, length, kv_heads, head_dim)  36.3 us
    psum x1, waiting for transfers between devices, body(): lax.psum(projected.astype(jnp.bfloat16), 'tensor').astype(jnp.float32)  35.3 us
    unnamed x16, local copies, waits for them, and re-layouts  26.8 us
    dot_general x2, matrix products, attend(): jnp.einsum('nkgd,ntkd->nkgt', query_block, block_keys, preferred_element_...  13.8 us
    dot_general x2, matrix products, attend(): jnp.einsum('nkgt,ntkd->nkgd', weight.astype(jnp.bfloat16), block_values,...  13.5 us
    reduce_scatter x1, waiting for transfers between devices, body(): lax.psum_scatter(mixtures.astype(jnp.bfloat16), 'seq', scatter_dimension=...  13 us
    slice x1, local copies, waits for them, and re-layouts, attend(): block_keys = block[:, 0].reshape(count, length, kv_heads, head_dim)  13 us
    another operation x1, local copies, waits for them, and re-layouts, attend(): block_values = block[:, 1].reshape(count, length, kv_heads, head_dim)  12 us
  transfers between devices with their start and end apart: 3, of which 2 were waited for; matrix products, arithmetic and copies ran while one was open for 26% of the time, Pallas kernels for 0%

commit v1 on v0

--- a/solution.py
+++ b/solution.py
@@ -1,7 +1,10 @@
 import jax
 import jax.numpy as jnp
 from jax import lax
+from jax.experimental import pallas as pl
+from jax.experimental.pallas import tpu as pltpu
 from jax.sharding import PartitionSpec as P
+import functools
 
 D = 4608
 H = 32
@@ -55,7 +58,7 @@
     return (totals, mixtures.reshape(count, -1))
 
 
-def body(
+def plain_body(
     hidden,
     pre_gain,
     w_query,
@@ -172,9 +175,470 @@
     return (layer_out, fresh_cache)
 
 
+MESH = pl.DeviceIdType.MESH
+VMEM_BYTES = 60 * 1024 * 1024
+
+
+def greet(axes):
+    barrier = pltpu.get_barrier_semaphore()
+    amount = 0
+    for axis, size in axes:
+        me = lax.axis_index(axis)
+        for offset in range(1, size):
+            peer = lax.rem(me + offset, size)
+            pl.semaphore_signal(barrier, inc=1, device_id={axis: peer}, device_id_type=MESH)
+            amount += 1
+    return barrier, amount
+
+
+def rope_lanes(x, cosine, sines):
+    return x * cosine + pltpu.roll(x, x.shape[-1] // 2, 1) * sines
+
+
+def project_kernel(
+    seq, chunk, hidden, gain, cosine, sines, w_query, w_key, w_value,
+    queries_out, fresh_out,
+    normed, gathered, own_query, acc_q, acc_k, acc_v, q_buf, k_buf, v_buf,
+    q_sem, k_sem, v_sem, send_sem, recv_sem,
+):
+    me = lax.axis_index("seq")
+    rows, depth = hidden.shape
+    steps = depth // chunk
+    weights = ((w_query, q_buf, q_sem), (w_key, k_buf, k_sem), (w_value, v_buf, v_sem))
+
+    def copy_of(which, step):
+        src, dst, sem = weights[which]
+        span = pl.ds(step * chunk, chunk)
+        return pltpu.make_async_copy(src.at[span], dst.at[span], sem.at[step])
+
+    for which in range(3):
+        for step in range(steps):
+            copy_of(which, step).start()
+    barrier, amount = greet((("seq", seq),))
+    x = hidden[...].astype(jnp.float32)
+    mean_square = jnp.mean(x * x, axis=-1, keepdims=True)
+    normed[...] = (x * lax.rsqrt(mean_square + 1e-06) * gain[...]).astype(jnp.bfloat16)
+
+    def product(which, buf, acc):
+        acc[...] = jnp.zeros_like(acc)
+
+        def one(step, carry):
+            copy_of(which, step).wait()
+            start = pl.multiple_of(step * chunk, chunk)
+            acc[...] += jnp.dot(
+                normed[:, pl.ds(start, chunk)],
+                buf[pl.ds(start, chunk), :],
+                preferred_element_type=jnp.float32,
+            )
+            return carry
+
+        lax.fori_loop(0, steps, one, 0)
+
+    product(0, q_buf, acc_q)
+    cos_all = cosine[...]
+    sin_all = sines[...]
+    hd = cos_all.shape[1]
+    for h in range(acc_q.shape[1] // hd):
+        lanes = slice(h * hd, (h + 1) * hd)
+        own_query[:, lanes] = rope_lanes(acc_q[:, lanes], cos_all, sin_all).astype(jnp.bfloat16)
+    pl.semaphore_wait(barrier, amount)
+    copies = []
+    for offset in range(1, seq):
+        peer = lax.rem(me + offset, seq)
+        copy = pltpu.make_async_remote_copy(
+            src_ref=own_query,
+            dst_ref=gathered.at[offset - 1],
+            send_sem=send_sem.at[offset - 1],
+            recv_sem=recv_sem.at[offset - 1],
+            device_id={"seq": peer},
+            device_id_type=MESH,
+        )
+        copy.start()
+        copies.append(copy)
+    product(1, k_buf, acc_k)
+    for h in range(acc_k.shape[1] // hd):
+        lanes = slice(h * hd, (h + 1) * hd)
+        fresh_out[0, :, lanes] = rope_lanes(acc_k[:, lanes], cos_all, sin_all).astype(jnp.bfloat16)
+    product(2, v_buf, acc_v)
+    fresh_out[1] = acc_v[...].astype(jnp.bfloat16)
+    queries_out[pl.ds(me, 1)] = own_query[...][None]
+    for offset in range(1, seq):
+        copies[offset - 1].wait()
+        source = lax.rem(me + seq - offset, seq)
+        queries_out[pl.ds(source, 1)] = gathered[pl.ds(offset - 1, 1)]
+
+
+def project(seq, hidden, gain, cosine, sines, w_query, w_key, w_value):
+    rows, depth = hidden.shape
+    q_width, kv_width = w_query.shape[1], w_key.shape[1]
+    chunk = 512 if depth % 512 == 0 else depth
+    steps = depth // chunk
+    vmem = pl.BlockSpec(memory_space=pltpu.VMEM)
+    hbm = pl.BlockSpec(memory_space=pl.ANY)
+    return pl.pallas_call(
+        functools.partial(project_kernel, seq, chunk),
+        out_shape=(
+            jax.ShapeDtypeStruct((seq, rows, q_width), jnp.bfloat16),
+            jax.ShapeDtypeStruct((2, rows, kv_width), jnp.bfloat16),
+        ),
+        in_specs=[vmem] * 4 + [hbm] * 3,
+        out_specs=(vmem, vmem),
+        scratch_shapes=[
+            pltpu.VMEM((rows, depth), jnp.bfloat16),
+            pltpu.VMEM((seq - 1, rows, q_width), jnp.bfloat16),
+            pltpu.VMEM((rows, q_width), jnp.bfloat16),
+            pltpu.VMEM((rows, q_width), jnp.float32),
+            pltpu.VMEM((rows, kv_width), jnp.float32),
+            pltpu.VMEM((rows, kv_width), jnp.float32),
+            pltpu.VMEM((depth, q_width), jnp.bfloat16),
+            pltpu.VMEM((depth, kv_width), jnp.bfloat16),
+            pltpu.VMEM((depth, kv_width), jnp.bfloat16),
+            pltpu.SemaphoreType.DMA((steps,)),
+            pltpu.SemaphoreType.DMA((steps,)),
+            pltpu.SemaphoreType.DMA((steps,)),
+            pltpu.SemaphoreType.DMA((seq - 1,)),
+            pltpu.SemaphoreType.DMA((seq - 1,)),
+        ],
+        compiler_params=pltpu.CompilerParams(
+            collective_id=0, has_side_effects=True, vmem_limit_bytes=VMEM_BYTES
+        ),
+    )(hidden, gain, cosine, sines, w_query, w_key, w_value)
+
+
+PAGES = 8
+ITEMS = 8
+
+
+def attend_kernel(
+    score_scale, max_blocks, codes, lengths, tasks, queries, pool, prompts,
+    packed,
+    q_heads, acc_w, acc_m, pool_buf, prompt_buf, item_req, item_task, pool_sem, prompt_sem,
+):
+    pages, _, block_len, kv_width = pool.shape
+    n_tasks, _, prompt_len, _ = prompts.shape
+    requests, heads, hd = q_heads.shape
+    kv_heads = kv_width // hd
+    group = heads // kv_heads
+    seq_index = lax.axis_index("seq")
+    batches = pages // PAGES
+
+    def pool_copy(b):
+        span = pl.ds(b * PAGES, PAGES)
+        return pltpu.make_async_copy(pool.at[span], pool_buf.at[span], pool_sem.at[b])
+
+    prompt_copy = pltpu.make_async_copy(prompts, prompt_buf, prompt_sem.at[0])
+    for b in range(batches):
+        pool_copy(b).start()
+    prompt_copy.start()
+    for h in range(heads):
+        q_heads[:, h, :] = queries[:, h * hd : (h + 1) * hd].astype(jnp.float32)
+    acc_w[...] = jnp.zeros_like(acc_w)
+    acc_m[...] = jnp.zeros_like(acc_m)
+
+    def list_one(r, count):
+        local = tasks[r] - seq_index * n_tasks
+        owned = (local >= 0) & (local < n_tasks)
+        item_req[count] = r
+        item_task[count] = jnp.clip(local, 0, n_tasks - 1)
+        return count + jnp.where(owned, 1, 0)
+
+    count = lax.fori_loop(0, requests, list_one, jnp.int32(0))
+
+    head_of = lax.broadcasted_iota(jnp.int32, (heads, hd), 0) // group
+    head_masks = [(head_of == g).astype(jnp.float32) for g in range(kv_heads)]
+
+    def batch(parts):
+        raws = []
+        for owner, valid, keys, values, length in parts:
+            q = q_heads[owner]
+            wide = jnp.concatenate([q * m for m in head_masks], axis=1).astype(jnp.bfloat16)
+            raws.append(
+                lax.dot_general(
+                    wide, keys(), (((1,), (1,)), ((), ())), preferred_element_type=jnp.float32
+                )
+            )
+        weights = []
+        for raw, (owner, valid, keys, values, length) in zip(raws, parts):
+            token = lax.broadcasted_iota(jnp.int32, raw.shape, 1)
+            weight = jnp.exp(cap_limit * jnp.tanh(raw * (score_scale / cap_limit)))
+            weights.append(jnp.where(token < valid, weight, 0.0))
+        mixed = []
+        for weight, (owner, valid, keys, values, length) in zip(weights, parts):
+            wide = jnp.dot(
+                weight.astype(jnp.bfloat16), values(), preferred_element_type=jnp.float32
+            )
+            mix = wide[:, :hd] * head_masks[0]
+            for g in range(1, kv_heads):
+                mix += wide[:, g * hd : (g + 1) * hd] * head_masks[g]
+            mixed.append(mix)
+        for weight, mix, (owner, valid, keys, values, length) in zip(weights, mixed, parts):
+            acc_w[owner, :, :length] += weight
+            acc_m[owner] += mix
+
+    def page_batch(b, carry):
+        pool_copy(b).wait()
+        parts = []
+        for i in range(PAGES):
+            p = b * PAGES + i
+            code = codes[p]
+            entry = jnp.maximum(code - 1, 0)
+            owner = entry // max_blocks
+            number = entry - owner * max_blocks
+            valid = jnp.where(code > 0, lengths[owner] - number * block_len, 0)
+            parts.append(
+                (owner, valid, lambda p=p: pool_buf[p, 0], lambda p=p: pool_buf[p, 1], block_len)
+            )
+        batch(parts)
+        return carry
+
+    lax.fori_loop(0, batches, page_batch, 0)
+    prompt_copy.wait()
+
+    def item_batch(b, carry):
+        parts = []
+        for i in range(ITEMS):
+            j = b * ITEMS + i
+            live = j < count
+            where = jnp.where(live, j, 0)
+            owner = item_req[where]
+            t = item_task[where]
+            valid = jnp.where(live, prompt_len, 0)
+            parts.append(
+                (
+                    owner, valid, lambda t=t: prompt_buf[t, 0], lambda t=t: prompt_buf[t, 1],
+                    prompt_len,
+                )
+            )
+        batch(parts)
+        return carry
+
+    lax.fori_loop(0, (count + ITEMS - 1) // ITEMS, item_batch, 0)
+    lane = lax.broadcasted_iota(jnp.int32, (requests, hd), 1)
+    totals = jnp.zeros((requests, hd), jnp.float32)
+    for h in range(heads):
+        packed[:, h * hd : (h + 1) * hd] = acc_m[:, h, :].astype(jnp.bfloat16)
+        totals = jnp.where(lane == h, jnp.sum(acc_w[:, h, :], axis=1, keepdims=True), totals)
+    packed[:, heads * hd :] = totals.astype(jnp.bfloat16)
+
+
+def attend_local(score_scale, max_blocks, codes, lengths, tasks, queries, pool, prompts, hd):
+    requests, q_width = queries.shape
+    heads = q_width // hd
+    smem = pl.BlockSpec(memory_space=pltpu.SMEM)
+    vmem = pl.BlockSpec(memory_space=pltpu.VMEM)
+    hbm = pl.BlockSpec(memory_space=pl.ANY)
+    return pl.pallas_call(
+        functools.partial(attend_kernel, score_scale, max_blocks),
+        out_shape=jax.ShapeDtypeStruct((requests, q_width + hd), jnp.bfloat16),
+        in_specs=[smem, smem, smem, vmem, hbm, hbm],
+        out_specs=vmem,
+        scratch_shapes=[
+            pltpu.VMEM((requests, heads, hd), jnp.float32),
+            pltpu.VMEM((requests, heads, hd), jnp.float32),
+            pltpu.VMEM((requests, heads, hd), jnp.float32),
+            pltpu.VMEM(pool.shape, pool.dtype),
+            pltpu.VMEM(prompts.shape, prompts.dtype),
+            pltpu.SMEM((requests + 1,), jnp.int32),
+            pltpu.SMEM((requests + 1,), jnp.int32),
+            pltpu.SemaphoreType.DMA((pool.shape[0] // PAGES,)),
+            pltpu.SemaphoreType.DMA((1,)),
+        ],
+        compiler_params=pltpu.CompilerParams(vmem_limit_bytes=VMEM_BYTES),
+    )(codes, lengths, tasks, queries, pool, prompts)
+
+
+def output_kernel(
+    seq, tensor, score_scale, hd, packed, queries, fresh, hidden, gain, w_out,
+    out,
+    landed, attended, w_buf, sent, arrived, square, squares,
+    w_sem, mix_send, mix_recv, part_send, part_recv, square_send, square_recv,
+):
+    me = lax.axis_index("seq")
+    mine = lax.axis_index("tensor")
+    rows, cols = out.shape
+    order = [(tensor // 2 + i) % tensor for i in range(tensor)]
+    order = [o for o in order if o] + [0]
+
+    def w_copy(offset):
+        c = lax.rem(mine + offset, tensor)
+        start = pl.multiple_of(c * cols, 128)
+        return pltpu.make_async_copy(
+            w_out.at[:, pl.ds(start, cols)], w_buf.at[offset], w_sem.at[offset]
+        )
+
+    barrier, amount = greet((("seq", seq), ("tensor", tensor)))
+    for offset in order:
+        w_copy(offset).start()
+    pl.semaphore_wait(barrier, amount)
+    copies = []
+    for offset in range(1, seq):
+        peer = lax.rem(me + offset, seq)
+        copy = pltpu.make_async_remote_copy(
+            src_ref=packed.at[peer],
+            dst_ref=landed.at[offset - 1],
+            send_sem=mix_send.at[offset - 1],
+            recv_sem=mix_recv.at[offset - 1],
+            device_id={"seq": peer},
+            device_id_type=MESH,
+        )
+        copy.start()
+        copies.append(copy)
+    q_width = queries.shape[2]
+    heads = q_width // hd
+    kv_width = fresh.shape[2]
+    group = heads // (kv_width // hd)
+    self_weights = []
+    for h in range(heads):
+        g = h // group
+        q = queries[me, :, h * hd : (h + 1) * hd].astype(jnp.float32)
+        k = fresh[0, :, g * hd : (g + 1) * hd].astype(jnp.float32)
+        raw = jnp.sum(q * k, axis=1, keepdims=True)
+        self_weights.append(jnp.exp(cap_limit * jnp.tanh(raw * (score_scale / cap_limit))))
+    for copy in copies:
+        copy.wait()
+    for h in range(heads):
+        g = h // group
+        lanes = slice(h * hd, (h + 1) * hd)
+        spot = slice(q_width + h, q_width + h + 1)
+        mix = packed[me, :, lanes].astype(jnp.float32)
+        total = packed[me, :, q_width:].astype(jnp.float32)
+        for s in range(seq - 1):
+            mix += landed[s, :, lanes].astype(jnp.float32)
+            total += landed[s, :, q_width:].astype(jnp.float32)
+        total = total[:, h : h + 1] + self_weights[h]
+        rounded = self_weights[h].astype(jnp.bfloat16).astype(jnp.float32)
+        mix += rounded * fresh[1, :, g * hd : (g + 1) * hd].astype(jnp.float32)
+        attended[:, lanes] = (mix / total).astype(jnp.bfloat16)
+    parts = []
+    for offset in order:
+        w_copy(offset).wait()
+        projected = jnp.dot(attended[...], w_buf[offset], preferred_element_type=jnp.float32)
+        if offset:
+            sent[offset - 1] = projected.astype(jnp.bfloat16)
+            copy = pltpu.make_async_remote_copy(
+                src_ref=sent.at[offset - 1],
+                dst_ref=arrived.at[offset - 1],
+                send_sem=part_send.at[offset - 1],
+                recv_sem=part_recv.at[offset - 1],
+                device_id={"tensor": lax.rem(mine + offset, tensor)},
+                device_id_type=MESH,
+            )
+            copy.start()
+            parts.append(copy)
+    whole = projected
+    for copy in parts:
+        copy.wait()
+    for s in range(tensor - 1):
+        whole += arrived[s].astype(jnp.float32)
+    part_square = jnp.sum(whole * whole, axis=1, keepdims=True)
+    square[...] = jnp.broadcast_to(part_square, square.shape)
+    copies = []
+    for offset in range(1, tensor):
+        copy = pltpu.make_async_remote_copy(
+            src_ref=square,
+            dst_ref=squares.at[offset - 1],
+            send_sem=square_send.at[offset - 1],
+            recv_sem=square_recv.at[offset - 1],
+            device_id={"tensor": lax.rem(mine + offset, tensor)},
+            device_id_type=MESH,
+        )
+        copy.start()
+        copies.append(copy)
+    start = pl.multiple_of(mine * cols, 128)
+    residual = hidden[:, pl.ds(start, cols)].astype(jnp.float32)
+    scaled = whole * gain[...]
+    for copy in copies:
+        copy.wait()
+    total_square = square[...]
+    for s in range(tensor - 1):
+        total_square += squares[s]
+    factor = lax.rsqrt(total_square[:, :1] / (cols * tensor) + 1e-06)
+    out[...] = (residual + scaled * factor).astype(jnp.bfloat16)
+
+
+def output_stage(seq, tensor, score_scale, hd, packed, queries, fresh, hidden, gain, w_out):
+    rows = hidden.shape[0]
+    cols = gain.shape[1]
+    depth = w_out.shape[0]
+    vmem = pl.BlockSpec(memory_space=pltpu.VMEM)
+    hbm = pl.BlockSpec(memory_space=pl.ANY)
+    dma = pltpu.SemaphoreType.DMA
+    return pl.pallas_call(
+        functools.partial(output_kernel, seq, tensor, score_scale, hd),
+        out_shape=jax.ShapeDtypeStruct((rows, cols), jnp.bfloat16),
+        in_specs=[vmem] * 5 + [hbm],
+        out_specs=vmem,
+        scratch_shapes=[
+            pltpu.VMEM((seq - 1, rows, packed.shape[2]), jnp.bfloat16),
+            pltpu.VMEM((rows, depth), jnp.bfloat16),
+            pltpu.VMEM((tensor, depth, cols), jnp.bfloat16),
+            pltpu.VMEM((tensor - 1, rows, cols), jnp.bfloat16),
+            pltpu.VMEM((tensor - 1, rows, cols), jnp.bfloat16),
+            pltpu.VMEM((rows, 128), jnp.float32),
+            pltpu.VMEM((tensor - 1, rows, 128), jnp.float32),
+            dma((tensor,)),
+            dma((seq - 1,)),
+            dma((seq - 1,)),
+            dma((tensor - 1,)),
+            dma((tensor - 1,)),
+            dma((tensor - 1,)),
+            dma((tensor - 1,)),
+        ],
+        compiler_params=pltpu.CompilerParams(
+            collective_id=1, has_side_effects=True, vmem_limit_bytes=VMEM_BYTES
+        ),
+    )(packed, queries, fresh, hidden, gain, w_out)
+
+
+def body(
+    seq, tensor, hidden, pre_gain, w_query, w_key, w_value, w_out, post_gain,
+    cache_pool, prompt_cache, task_ids, cache_lengths, block_table,
+):
+    seq_index = lax.axis_index("seq")
+    own_rows = hidden.shape[0]
+    requests = task_ids.shape[0]
+    pages_dev = cache_pool.shape[0]
+    kv_width = cache_pool.shape[3]
+    prompt_len = prompt_cache.shape[2]
+    score_scale = float(D // H) ** (-0.5)
+    own_lengths = lax.dynamic_slice_in_dim(cache_lengths, seq_index * own_rows, own_rows)
+    half = HD // 2
+    frequency = 10000.0 ** (-jnp.arange(half, dtype=jnp.float32) / half)
+    angles = (prompt_len + own_lengths).astype(jnp.float32)[:, None] * frequency[None, :]
+    cosine = jnp.cos(angles)
+    sines = jnp.sin(angles)
+    cosine = jnp.concatenate([cosine, cosine], axis=1)
+    sines = jnp.concatenate([-sines, sines], axis=1)
+    page_ids = seq_index * pages_dev + jnp.arange(pages_dev)
+    flat_table = block_table.reshape(-1)
+    matches = flat_table[None, :] == page_ids[:, None]
+    entry = jnp.arange(1, flat_table.shape[0] + 1)
+    codes = jnp.sum(jnp.where(matches, entry[None, :], 0), axis=1)
+    queries, fresh = project(
+        seq, hidden, pre_gain[None], cosine, sines, w_query, w_key, w_value
+    )
+    packed = attend_local(
+        score_scale, block_table.shape[1], codes, cache_lengths, task_ids,
+        queries.reshape(requests, -1), cache_pool, prompt_cache, HD,
+    )
+    layer_out = output_stage(
+        seq, tensor, score_scale, HD, packed.reshape(seq, own_rows, -1), queries, fresh,
+        hidden, post_gain[None], w_out,
+    )
+    return (layer_out, jnp.swapaxes(fresh, 0, 1))
+
+
 def solution(mesh):
+    seq, tensor = mesh.shape["seq"], mesh.shape["tensor"]
+
+    def chosen(*arrays):
+        cols, heads, pages = arrays[6].shape[0], arrays[2].shape[1] // HD, arrays[7].shape[0]
+        if cols % 128 or heads % 8 or pages % PAGES or seq < 2 or tensor < 2:
+            return plain_body(*arrays)
+        return body(seq, tensor, *arrays)
+
     return jax.shard_map(
-        body,
+        chosen,
         mesh=mesh,
         in_specs=(
             P(("groups", "seq"), None),

time: 240 us -> 57.1 us (0.24); the launches traced: 238 us -> 57.3 us
  local copies, waits for them, and re-layouts: 113 us -> 4.35 us
  Pallas kernels: 0 us -> 49.9 us
  waiting for transfers between devices: 48.4 us -> 0 us
  matrix products: 47.2 us -> 0 us
  between operations: 14 us -> 0.72 us
  blocking collectives: 7.22 us -> 0 us
  other arithmetic: 7.5 us -> 2.38 us
    pallas_call x0 -> x3, Pallas kernels: none -> 49.9 us  [the longest x1 23.4 us: output_stage(): pl.pallas_call(functools.partial(output_kernel, seq, tensor, score_scale,...]
    slice x4 -> x0, local copies, waits for them, and re-layouts: 49.3 us -> none  [the longest x3 36.3 us: attend(): block_values = block[:, 1].reshape(count, length, kv_heads, head_dim)]
    dot_general x11 -> x0, matrix products: 47.2 us -> none  [the longest x2 13.8 us: attend(): jnp.einsum('nkgd,ntkd->nkgt', query_block, block_keys, preferred_element_...]
    psum x1 -> x0, waiting for transfers between devices: 35.3 us -> none  [body(): lax.psum(projected.astype(jnp.bfloat16), 'tensor').astype(jnp.float32)]
    unnamed x16 -> x9, local copies, waits for them, and re-layouts: 26.8 us -> 2.33 us
    another operation x2 -> x0, local copies, waits for them, and re-layouts: 24 us -> none  [the longest x1 12 us: attend(): block_values = block[:, 1].reshape(count, length, kv_heads, head_dim)]
    reduce_scatter x1 -> x0, waiting for transfers between devices: 13 us -> none  [body(): lax.psum_scatter(mixtures.astype(jnp.bfloat16), 'seq', scatter_dimension=...]
    gather x1 -> x0, local copies, waits for them, and re-layouts: 11.2 us -> none  [body(): task_rows = prompt_cache[jnp.clip(local_task, 0, tasks_dev - 1)]]
  transfers between devices with their start and end apart: 3 -> 0, of which waited for: 2 -> 0; matrix products, arithmetic and copies ran while one was open for 26% -> 0% of each run, Pallas kernels for 0% -> 0%
where the time goes in v1:
time: 57.1 us; the launch traced here: 57.3 us
  Pallas kernels  49.9 us (87%)
  local copies, waits for them, and re-layouts  4.35 us (8%)
  other arithmetic  2.38 us (4%)
  between operations  0.72 us (1%)
    pallas_call x1, Pallas kernels, output_stage(): pl.pallas_call(functools.partial(output_kernel, seq, tensor, score_scale,...  23.4 us
    pallas_call x1, Pallas kernels, project(): pl.pallas_call(functools.partial(project_kernel, seq, chunk), out_shape=(...  14.3 us
    pallas_call x1, Pallas kernels, attend_local(): pl.pallas_call(functools.partial(attend_kernel, score_scale, max_blocks),...  12.2 us
    unnamed x9, local copies, waits for them, and re-layouts  2.33 us
    broadcast_in_dim x1, local copies, waits for them, and re-layouts, body(): pre_gain[None]  1.35 us

profile of v1, /device:TPU:0, one launch (start us, length us, event | category | flops | bytes accessed | tf_op | source)
XLA Modules:
  0.0 57.3 jit_solution(17442337236242443335)
XLA Ops:
  0.6 0.7 %add_convert_fusion = f32[32]{0:T(128)S(1)} fusion(s32[128]{0:T(128)} %lengths.1, s32[]{:T(128)S(6)} %select_n.8), kind=kLoop, calls=%fused_computation.8 | loop fusion | flops 64 | bytes 260 | tf_op jit(solution)/shard_map/convert_element_type | solution.py:607
  1.4 0.1 fusion
  1.5 0.7 %pad_maximum_fusion = (f32[32,128]{1,0:T(8,128)}, f32[32,128]{1,0:T(8,128)}) fusion(f32[32,64]{1,0:T(8,128)S(1)} %get-tuple-element.14, f32[32,64]{1,0:T(8,128)S(1)} %get-tuple-element.13, f32[32,64]{1,0:T(8,128)S(1)} %get-tuple-element.12), kind=kLoop, calls=%fused_computation.3 | loop fusion | flops 8192 | bytes 57344 | tf_op jit(solution)/shard_map/concatenate | solution.py:610
  2.2 1.3 %broadcast_in_dim.24.gain = f32[1,4608]{1,0:T(1,128)} reshape(f32[4608]{0:T(1024)} %param.13) | data formatting | bytes 36864 | tf_op jit(solution)/shard_map/broadcast_in_dim | solution.py:618
  3.6 0.0 copy-start.1
  3.6 14.3 %shard_map.131 = (bf16[4,32,1024]{2,1,0:T(8,128)(2,1)}, bf16[2,32,512]{2,1,0:T(8,128)(2,1)}) custom-call(bf16[32,4608]{1,0:T(8,128)(2,1)} %hidden.3, f32[1,4608]{1,0:T(1,128)} %broadcast_in_dim.24.gain, f32[32,128]{1,0:T(8,128)} %get-tuple-element.15.cosine, f32[32,128]{1,0:T(8,128)} %get-tuple-element.16.sines, bf16[4608,1024]{1,0:T(8,128)(2,1)} %w_query.1, ...), custom_call_target="tpu_custom_call" | custom-call | tf_op jit(solution)/shard_map/pallas_call | solution.py:278
  17.9 0.0 copy-done.1
  17.9 0.1 copy.17
  18.0 0.1 eq.15
  18.1 0.8 %select_reduce_fusion.codes = s32[64]{0:T(128)} fusion(s32[4096]{0:T(1024)S(1)} %iota_add_fusion, s32[4096]{0:T(1024)S(1)} %eq.15, s32[64]{0:T(128)S(1)} %iota_add_fusion.1), kind=kLoop, calls=%fused_computation | loop fusion | flops 786368 | bytes 33280 | tf_op jit(solution)/shard_map/reduce_sum | solution.py:616
  18.9 0.0 copy-start.2
  18.9 12.2 %shard_map.132 = bf16[128,1152]{1,0:T(8,128)(2,1)} custom-call(s32[64]{0:T(128)} %select_reduce_fusion.codes, s32[128]{0:T(128)} %lengths.1, s32[128]{0:T(128)} %tasks.1, bf16[128,1024]{1,0:T(8,128)(2,1)} %bitcast.4, bf16[64,2,128,512]{3,2,1,0:T(8,128)(2,1)} %pool.1, bf16[64,2,64,512]{3,2,1,0:T(8,128)(2,1)} %prompts.1), custom_call_target="tpu_custom_call" | custom-call | tf_op jit(solution)/shard_map/pallas_call | solution.py:430
  31.1 0.0 copy-start
  31.1 0.0 copy-done.2
  31.1 0.6 %broadcast_in_dim.25.gain = f32[1,1152]{1,0:T(1,128)} reshape(f32[1152]{0:T(1024)S(1)} %copy-done.2) | data formatting | bytes 9216 | tf_op jit(solution)/shard_map/broadcast_in_dim | solution.py:626
  31.7 23.4 %shard_map.133 = bf16[32,1152]{1,0:T(8,128)(2,1)} custom-call(bf16[4,32,1152]{2,1,0:T(8,128)(2,1)} %bitcast.3, bf16[4,32,1024]{2,1,0:T(8,128)(2,1)} %get-tuple-element.4.queries, bf16[2,32,512]{2,1,0:T(8,128)(2,1)} %get-tuple-element.5.fresh, bf16[32,4608]{1,0:T(8,128)(2,1)} %hidden.3, f32[1,1152]{1,0:T(1,128)} %broadcast_in_dim.25.gain, ...), custom_call_target="tpu_custom_call" | custom-call | tf_op jit(solution)/shard_map/pallas_call | solution.py:566
  55.1 0.0 copy-done
  55.1 0.7 %copy.18 = bf16[32,2,512]{2,1,0:T(2,128)(2,1)} copy(bf16[32,2,512]{2,0,1:T(8,128)(2,1)S(1)} %bitcast.5) | data formatting | bytes 131072
  55.8 1.5 %copy.20 = bf16[32,1152]{1,0:T(8,128)(2,1)} copy(bf16[32,1152]{1,0:T(8,128)(2,1)} %shard_map.133) | data formatting | bytes 147456
  (3 shorter events, 0.0 us)
Async XLA Ops:
  3.6 14.4 %copy-start.1 = (s32[128,32]{0,1:T(8,128)S(1)}, s32[128,32]{0,1:T(8,128)}, u32[]{:S(2)}) copy-start(s32[128,32]{0,1:T(8,128)} %param.23) | copy-start | bytes 49156
  18.9 12.2 %copy-start.2 = (f32[1152]{0:T(1024)S(1)}, f32[1152]{0:T(1024)}, u32[]{:S(2)}) copy-start(f32[1152]{0:T(1024)} %param.18) | copy-start | bytes 13828
  31.1 24.0 %copy-start = (bf16[2,32,512]{2,1,0:T(8,128)(2,1)S(1)}, bf16[2,32,512]{2,1,0:T(8,128)(2,1)}, u32[]{:S(2)}) copy-start(bf16[2,32,512]{2,1,0:T(8,128)(2,1)} %get-tuple-element.5.fresh) | copy-start | bytes 196612

commit v2 on v1

--- a/solution.py
+++ b/solution.py
@@ -5,6 +5,7 @@
 from jax.experimental.pallas import tpu as pltpu
 from jax.sharding import PartitionSpec as P
 import functools
+import numpy as np
 
 D = 4608
 H = 32
@@ -196,7 +197,7 @@
 
 
 def project_kernel(
-    seq, chunk, hidden, gain, cosine, sines, w_query, w_key, w_value,
+    seq, chunk, prompt_len, lengths, hidden, gain, frequency, w_query, w_key, w_value,
     queries_out, fresh_out,
     normed, gathered, own_query, acc_q, acc_k, acc_v, q_buf, k_buf, v_buf,
     q_sem, k_sem, v_sem, send_sem, recv_sem,
@@ -217,7 +218,7 @@
     barrier, amount = greet((("seq", seq),))
     x = hidden[...].astype(jnp.float32)
     mean_square = jnp.mean(x * x, axis=-1, keepdims=True)
-    normed[...] = (x * lax.rsqrt(mean_square + 1e-06) * gain[...]).astype(jnp.bfloat16)
+    normed[...] = (x * lax.rsqrt(mean_square + 1e-06) * gain[...][None]).astype(jnp.bfloat16)
 
     def product(which, buf, acc):
         acc[...] = jnp.zeros_like(acc)
@@ -234,10 +235,17 @@
 
         lax.fori_loop(0, steps, one, 0)
 
+    hd = frequency.shape[1]
+    row = lax.broadcasted_iota(jnp.int32, (rows, hd), 0)
+    position = jnp.zeros((rows, hd), jnp.int32)
+    for i in range(rows):
+        position = jnp.where(row == i, lengths[me * rows + i] + prompt_len, position)
+    angles = position.astype(jnp.float32) * frequency[...]
+    lane = lax.broadcasted_iota(jnp.int32, (rows, hd), 1)
+    cos_all = jnp.cos(angles)
+    sin_all = jnp.sin(angles)
+    sin_all = jnp.where(lane < hd // 2, -sin_all, sin_all)
     product(0, q_buf, acc_q)
-    cos_all = cosine[...]
-    sin_all = sines[...]
-    hd = cos_all.shape[1]
     for h in range(acc_q.shape[1] // hd):
         lanes = slice(h * hd, (h + 1) * hd)
         own_query[:, lanes] = rope_lanes(acc_q[:, lanes], cos_all, sin_all).astype(jnp.bfloat16)
@@ -268,7 +276,7 @@
         queries_out[pl.ds(source, 1)] = gathered[pl.ds(offset - 1, 1)]
 
 
-def project(seq, hidden, gain, cosine, sines, w_query, w_key, w_value):
+def project(seq, prompt_len, lengths, hidden, gain, frequency, w_query, w_key, w_value):
     rows, depth = hidden.shape
     q_width, kv_width = w_query.shape[1], w_key.shape[1]
     chunk = 512 if depth % 512 == 0 else depth
@@ -276,12 +284,12 @@
     vmem = pl.BlockSpec(memory_space=pltpu.VMEM)
     hbm = pl.BlockSpec(memory_space=pl.ANY)
     return pl.pallas_call(
-        functools.partial(project_kernel, seq, chunk),
+        functools.partial(project_kernel, seq, chunk, prompt_len),
         out_shape=(
             jax.ShapeDtypeStruct((seq, rows, q_width), jnp.bfloat16),
             jax.ShapeDtypeStruct((2, rows, kv_width), jnp.bfloat16),
         ),
-        in_specs=[vmem] * 4 + [hbm] * 3,
+        in_specs=[pl.BlockSpec(memory_space=pltpu.SMEM)] + [vmem] * 3 + [hbm] * 3,
         out_specs=(vmem, vmem),
         scratch_shapes=[
             pltpu.VMEM((rows, depth), jnp.bfloat16),
@@ -302,7 +310,7 @@
         compiler_params=pltpu.CompilerParams(
             collective_id=0, has_side_effects=True, vmem_limit_bytes=VMEM_BYTES
         ),
-    )(hidden, gain, cosine, sines, w_query, w_key, w_value)
+    )(lengths, hidden, gain, frequency, w_query, w_key, w_value)
 
 
 PAGES = 8
@@ -310,9 +318,9 @@
 
 
 def attend_kernel(
-    score_scale, max_blocks, codes, lengths, tasks, queries, pool, prompts,
-    packed,
-    q_heads, acc_w, acc_m, pool_buf, prompt_buf, item_req, item_task, pool_sem, prompt_sem,
+    score_scale, max_blocks, codes, lengths, tasks, queries, fresh, pool, prompts,
+    packed, fresh_out,
+    fresh_rows, used, q_heads, acc_w, acc_m, pool_buf, prompt_buf, item_req, item_task, pool_sem, prompt_sem,
 ):
     pages, _, block_len, kv_width = pool.shape
     n_tasks, _, prompt_len, _ = prompts.shape
@@ -326,23 +334,40 @@
         span = pl.ds(b * PAGES, PAGES)
         return pltpu.make_async_copy(pool.at[span], pool_buf.at[span], pool_sem.at[b])
 
-    prompt_copy = pltpu.make_async_copy(prompts, prompt_buf, prompt_sem.at[0])
+    def prompt_copy(t):
+        return pltpu.make_async_copy(prompts.at[t], prompt_buf.at[t], prompt_sem.at[t])
+
     for b in range(batches):
         pool_copy(b).start()
-    prompt_copy.start()
+
+    def clear_one(t, carry):
+        used[t] = 0
+        return carry
+
+    lax.fori_loop(0, n_tasks, clear_one, 0)
+    def list_one(r, count):
+        local = tasks[r] - seq_index * n_tasks
+        owned = (local >= 0) & (local < n_tasks)
+        local = jnp.clip(local, 0, n_tasks - 1)
+        item_req[count] = r
+        item_task[count] = local
+
+        @pl.when(owned & (used[local] == 0))
+        def _():
+            used[local] = 1
+            prompt_copy(local).start()
+
+        return count + jnp.where(owned, 1, 0)
+
+    count = lax.fori_loop(0, requests, list_one, jnp.int32(0))
+
     for h in range(heads):
         q_heads[:, h, :] = queries[:, h * hd : (h + 1) * hd].astype(jnp.float32)
     acc_w[...] = jnp.zeros_like(acc_w)
     acc_m[...] = jnp.zeros_like(acc_m)
-
-    def list_one(r, count):
-        local = tasks[r] - seq_index * n_tasks
-        owned = (local >= 0) & (local < n_tasks)
-        item_req[count] = r
-        item_task[count] = jnp.clip(local, 0, n_tasks - 1)
-        return count + jnp.where(owned, 1, 0)
-
-    count = lax.fori_loop(0, requests, list_one, jnp.int32(0))
+    for i in range(2):
+        fresh_rows[:, i, :] = fresh[i].astype(jnp.float32)
+    fresh_out[...] = fresh_rows[...].astype(jnp.bfloat16)
 
     head_of = lax.broadcasted_iota(jnp.int32, (heads, hd), 0) // group
     head_masks = [(head_of == g).astype(jnp.float32) for g in range(kv_heads)]
@@ -392,7 +417,15 @@
         return carry
 
     lax.fori_loop(0, batches, page_batch, 0)
-    prompt_copy.wait()
+
+    def wait_one(t, carry):
+        @pl.when(used[t] == 1)
+        def _():
+            prompt_copy(t).wait()
+
+        return carry
+
+    lax.fori_loop(0, n_tasks, wait_one, 0)
 
     def item_batch(b, carry):
         parts = []
@@ -421,7 +454,9 @@
     packed[:, heads * hd :] = totals.astype(jnp.bfloat16)
 
 
-def attend_local(score_scale, max_blocks, codes, lengths, tasks, queries, pool, prompts, hd):
+def attend_local(
+    score_scale, max_blocks, codes, lengths, tasks, queries, fresh, pool, prompts, hd
+):
     requests, q_width = queries.shape
     heads = q_width // hd
     smem = pl.BlockSpec(memory_space=pltpu.SMEM)
@@ -429,10 +464,15 @@
     hbm = pl.BlockSpec(memory_space=pl.ANY)
     return pl.pallas_call(
         functools.partial(attend_kernel, score_scale, max_blocks),
-        out_shape=jax.ShapeDtypeStruct((requests, q_width + hd), jnp.bfloat16),
-        in_specs=[smem, smem, smem, vmem, hbm, hbm],
-        out_specs=vmem,
+        out_shape=(
+            jax.ShapeDtypeStruct((requests, q_width + hd), jnp.bfloat16),
+            jax.ShapeDtypeStruct((fresh.shape[1], 2, fresh.shape[2]), jnp.bfloat16),
+        ),
+        in_specs=[smem, smem, smem, vmem, vmem, hbm, hbm],
+        out_specs=(vmem, vmem),
         scratch_shapes=[
+            pltpu.VMEM((fresh.shape[1], 2, fresh.shape[2]), jnp.float32),
+            pltpu.SMEM((prompts.shape[0],), jnp.int32),
             pltpu.VMEM((requests, heads, hd), jnp.float32),
             pltpu.VMEM((requests, heads, hd), jnp.float32),
             pltpu.VMEM((requests, heads, hd), jnp.float32),
@@ -441,14 +481,14 @@
             pltpu.SMEM((requests + 1,), jnp.int32),
             pltpu.SMEM((requests + 1,), jnp.int32),
             pltpu.SemaphoreType.DMA((pool.shape[0] // PAGES,)),
-            pltpu.SemaphoreType.DMA((1,)),
+            pltpu.SemaphoreType.DMA((prompts.shape[0],)),
         ],
         compiler_params=pltpu.CompilerParams(vmem_limit_bytes=VMEM_BYTES),
-    )(codes, lengths, tasks, queries, pool, prompts)
+    )(codes, lengths, tasks, queries, fresh, pool, prompts)
 
 
 def output_kernel(
-    seq, tensor, score_scale, hd, packed, queries, fresh, hidden, gain, w_out,
+    seq, tensor, score_scale, hd, packed, queries, fresh, gain, w_out,
     out,
     landed, attended, w_buf, sent, arrived, square, squares,
     w_sem, mix_send, mix_recv, part_send, part_recv, square_send, square_recv,
@@ -544,29 +584,27 @@
         )
         copy.start()
         copies.append(copy)
-    start = pl.multiple_of(mine * cols, 128)
-    residual = hidden[:, pl.ds(start, cols)].astype(jnp.float32)
-    scaled = whole * gain[...]
+    scaled = whole * gain[...][None]
     for copy in copies:
         copy.wait()
     total_square = square[...]
     for s in range(tensor - 1):
         total_square += squares[s]
     factor = lax.rsqrt(total_square[:, :1] / (cols * tensor) + 1e-06)
-    out[...] = (residual + scaled * factor).astype(jnp.bfloat16)
-
-
-def output_stage(seq, tensor, score_scale, hd, packed, queries, fresh, hidden, gain, w_out):
-    rows = hidden.shape[0]
-    cols = gain.shape[1]
+    out[...] = scaled * factor
+
+
+def output_stage(seq, tensor, score_scale, hd, packed, queries, fresh, gain, w_out):
+    rows = packed.shape[1]
+    cols = gain.shape[0]
     depth = w_out.shape[0]
     vmem = pl.BlockSpec(memory_space=pltpu.VMEM)
     hbm = pl.BlockSpec(memory_space=pl.ANY)
     dma = pltpu.SemaphoreType.DMA
     return pl.pallas_call(
         functools.partial(output_kernel, seq, tensor, score_scale, hd),
-        out_shape=jax.ShapeDtypeStruct((rows, cols), jnp.bfloat16),
-        in_specs=[vmem] * 5 + [hbm],
+        out_shape=jax.ShapeDtypeStruct((rows, cols), jnp.float32),
+        in_specs=[vmem] * 4 + [hbm],
         out_specs=vmem,
         scratch_shapes=[
             pltpu.VMEM((seq - 1, rows, packed.shape[2]), jnp.bfloat16),
@@ -587,7 +625,7 @@
         compiler_params=pltpu.CompilerParams(
             collective_id=1, has_side_effects=True, vmem_limit_bytes=VMEM_BYTES
         ),
-    )(packed, queries, fresh, hidden, gain, w_out)
+    )(packed, queries, fresh, gain, w_out)
 
 
 def body(
@@ -601,31 +639,30 @@
     kv_width = cache_pool.shape[3]
     prompt_len = prompt_cache.shape[2]
     score_scale = float(D // H) ** (-0.5)
-    own_lengths = lax.dynamic_slice_in_dim(cache_lengths, seq_index * own_rows, own_rows)
     half = HD // 2
-    frequency = 10000.0 ** (-jnp.arange(half, dtype=jnp.float32) / half)
-    angles = (prompt_len + own_lengths).astype(jnp.float32)[:, None] * frequency[None, :]
-    cosine = jnp.cos(angles)
-    sines = jnp.sin(angles)
-    cosine = jnp.concatenate([cosine, cosine], axis=1)
-    sines = jnp.concatenate([-sines, sines], axis=1)
+    frequency = 10000.0 ** (-np.arange(half) / half)
+    frequency = jnp.asarray(np.concatenate([frequency, frequency])[None], jnp.float32)
+    queries, fresh = project(
+        seq, prompt_len, cache_lengths, hidden, pre_gain, frequency, w_query, w_key, w_value
+    )
+    queries, fresh, block_table = lax.optimization_barrier((queries, fresh, block_table))
     page_ids = seq_index * pages_dev + jnp.arange(pages_dev)
     flat_table = block_table.reshape(-1)
     matches = flat_table[None, :] == page_ids[:, None]
     entry = jnp.arange(1, flat_table.shape[0] + 1)
     codes = jnp.sum(jnp.where(matches, entry[None, :], 0), axis=1)
-    queries, fresh = project(
-        seq, hidden, pre_gain[None], cosine, sines, w_query, w_key, w_value
-    )
-    packed = attend_local(
+    packed, fresh_cache = attend_local(
         score_scale, block_table.shape[1], codes, cache_lengths, task_ids,
-        queries.reshape(requests, -1), cache_pool, prompt_cache, HD,
-    )
-    layer_out = output_stage(
+        queries.reshape(requests, -1), fresh, cache_pool, prompt_cache, HD,
+    )
+    update = output_stage(
         seq, tensor, score_scale, HD, packed.reshape(seq, own_rows, -1), queries, fresh,
-        hidden, post_gain[None], w_out,
-    )
-    return (layer_out, jnp.swapaxes(fresh, 0, 1))
+        post_gain, w_out,
+    )
+    cols = post_gain.shape[0]
+    residual = lax.dynamic_slice_in_dim(hidden, lax.axis_index("tensor") * cols, cols, 1)
+    layer_out = (residual.astype(jnp.float32) + update).astype(jnp.bfloat16)
+    return (layer_out, fresh_cache)
 
 
 def solution(mesh):

time: 57.1 us -> 53.2 us (0.932); the launches traced: 57.3 us -> 52.8 us
  local copies, waits for them, and re-layouts: 4.35 us -> 0.18 us
    unnamed x9 -> x2, local copies, waits for them, and re-layouts: 2.33 us -> 0.01 us
    broadcast_in_dim x2 -> x0, local copies, waits for them, and re-layouts: 1.94 us -> none  [the longest x1 1.35 us: body(): pre_gain[None]]
    pallas_call x1, Pallas kernels: 23.4 us -> 22.3 us  [output_stage(): pl.pallas_call(functools.partial(output_kernel, seq, tensor, score_scale,...]
    convert_element_type x1, other arithmetic: 0.73 us -> 1.61 us  [body(): layer_out = (residual.astype(jnp.float32) + update).astype(jnp.bfloat16)]
    pallas_call x1, Pallas kernels: 12.2 us -> 12.9 us  [attend_local(): pl.pallas_call(functools.partial(attend_kernel, score_scale, max_blocks),...]
    concatenate x1 -> x0, other arithmetic: 0.69 us -> none  [body(): cosine = jnp.concatenate([cosine, cosine], axis=1)]
where the time goes in v2:
time: 53.2 us; the launch traced here: 52.8 us
  Pallas kernels  49.5 us (93%)
  other arithmetic  2.43 us (5%)
  between operations  0.69 us (1%)
    pallas_call x1, Pallas kernels, output_stage(): pl.pallas_call(functools.partial(output_kernel, seq, tensor, score_scale,...  22.3 us
    pallas_call x1, Pallas kernels, project(): pl.pallas_call(functools.partial(project_kernel, seq, chunk, prompt_len),...  14.4 us
    pallas_call x1, Pallas kernels, attend_local(): pl.pallas_call(functools.partial(attend_kernel, score_scale, max_blocks),...  12.9 us
    convert_element_type x1, other arithmetic, body(): layer_out = (residual.astype(jnp.float32) + update).astype(jnp.bfloat16)  1.61 us

profile of v2, /device:TPU:0, one launch (start us, length us, event | category | flops | bytes accessed | tf_op | source)
XLA Modules:
  0.0 52.8 jit_solution(11487499905112629349)
XLA Ops:
  0.7 0.0 copy-start
  0.7 14.4 %shard_map.140 = (bf16[4,32,1024]{2,1,0:T(8,128)(2,1)}, bf16[2,32,512]{2,1,0:T(8,128)(2,1)}) custom-call(s32[128]{0:T(128)} %lengths.3, bf16[32,4608]{1,0:T(8,128)(2,1)} %hidden.1, f32[4608]{0:T(1024)} %gain.2, f32[1,128]{1,0:T(1,128)} %constant.19.clone.frequency, bf16[4608,1024]{1,0:T(8,128)(2,1)} %w_query.1, bf16[4608,512]{1,0:T(8,128)(2,1)} %w_key.1, ...), custom_call_target="tpu_custom_call" | custom-call | tf_op jit(solution)/shard_map/pallas_call | solution.py:286
  15.0 0.0 copy-done
  15.1 0.1 copy.16
  15.1 0.1 eq.15
  15.2 0.8 %select_reduce_fusion.codes = s32[64]{0:T(128)} fusion(s32[4096]{0:T(1024)S(1)} %iota_add_fusion, s32[4096]{0:T(1024)S(1)} %eq.15, s32[64]{0:T(128)S(1)} %iota_add_fusion.1), kind=kLoop, calls=%fused_computation | loop fusion | flops 786368 | bytes 33280 | tf_op jit(solution)/shard_map/reduce_sum | solution.py:653
  16.0 12.9 %shard_map.141 = (bf16[128,1152]{1,0:T(8,128)(2,1)}, bf16[32,2,512]{2,1,0:T(2,128)(2,1)}) custom-call(s32[64]{0:T(128)} %select_reduce_fusion.codes, s32[128]{0:T(128)} %lengths.3, s32[128]{0:T(128)} %tasks.1, bf16[128,1024]{1,0:T(8,128)(2,1)} %bitcast.2, bf16[2,32,512]{2,1,0:T(8,128)(2,1)} %get-tuple-element.13.fresh, bf16[64,2,128,512]{3,2,1,0:T(8,128)(2,1)} %pool.1, ...), custom_call_target="tpu_custom_call" | custom-call | tf_op jit(solution)/shard_map/pallas_call | solution.py:465
  28.9 22.3 %shard_map.142 = f32[32,1152]{1,0:T(8,128)} custom-call(bf16[4,32,1152]{2,1,0:T(8,128)(2,1)} %bitcast.3, bf16[4,32,1024]{2,1,0:T(8,128)(2,1)} %get-tuple-element.12.queries, bf16[2,32,512]{2,1,0:T(8,128)(2,1)} %get-tuple-element.13.fresh, f32[1152]{0:T(1024)} %gain.3, bf16[1024,4608]{1,0:T(8,128)(2,1)} %w_out.1), custom_call_target="tpu_custom_call" | custom-call | tf_op jit(solution)/shard_map/pallas_call | solution.py:604
  51.2 1.6 %add_convert_fusion = bf16[32,1152]{1,0:T(8,128)(2,1)} fusion(f32[32,1152]{1,0:T(8,128)} %shard_map.142, bf16[32,4608]{1,0:T(8,128)(2,1)} %hidden.1, s32[]{:T(128)S(6)} %select_n.7), kind=kLoop, calls=%fused_computation.1 | loop fusion | flops 110592 | bytes 294916 | tf_op jit(solution)/shard_map/convert_element_type | solution.py:664
  (2 shorter events, 0.0 us)
Async XLA Ops:
  0.7 14.4 %copy-start = (s32[128,32]{0,1:T(8,128)S(1)}, s32[128,32]{0,1:T(8,128)}, u32[]{:S(2)}) copy-start(s32[128,32]{0,1:T(8,128)} %param.24) | copy-start | bytes 49156
